TPU v7x, 256 devices: a whole 4x4x8 slice. The times are simulated.
256 devices in a mesh: lat: 8 (over x, core), lon: 32 (over y, z).
Axes of the slice: x: 4, y: 4, z: 8, core: 2. Of those that a mesh axis runs over, the one named last changes fastest.
Arguments:
- prediction_fields: float32 [4, 69, 1440, 1024], P(None, None, 'lon', 'lat'), may hold values from -16 to 16
- verifying_state: float32 [69, 1440, 1024], P(None, 'lon', 'lat'), may hold values from -16 to 16
- normal_state: float32 [69, 1440, 1024], P(None, 'lon', 'lat'), may hold values from -16 to 16
- evaluated_point_flag: int32 [1440, 1024], P('lon', 'lat'), may hold values 0 or 1
- parallels_each_strip: int32 [8], replicated, may hold values from 1 to 128, 721 in all
Outputs:
- parallel_quadratic_error: float32 [4, 69, 1024], P(None, None, 'lat')
- parallel_systematic_error: float32 [4, 69, 1024], P(None, None, 'lat')
- parallel_pattern_skill: float32 [4, 69, 1024], P(None, None, 'lat')
- rmse: float32 [4, 69], replicated
- systematic_error: float32 [4, 69], replicated
- pattern_skill: float32 [4, 69], replicated
Inputs may be any that keep to these rules, and one draw needn't show every extreme that they name: `parallels_each_strip`: they sum to 721, and some band holds exactly 128 rows.
All inputs are finite; a program needn't handle non-finite values.
Results may differ from a plain program's by a relative error of at most 0.00002.
Values sent between devices are 32-bit elements.
A program may use at most 64 MiB of HBM per device.

v0:
```python
import functools
import jax
import jax.numpy as jnp
from jax import lax
from jax.sharding import Mesh
from jax.sharding import PartitionSpec as P

MEAN_ROWS = 90
LAT = ("lat_0", "lat_1")
LON = ("lon_0", "lon_1")
LAT_LON = ("lat_0", "lat_1", "lon_0", "lon_1")
minimum_divisor = 0.1


def by_axis(shard, axes):
    return functools.reduce(lax.psum, axes, shard)


def split_up(shard, dim, devices):
    dims = shard.shape
    tiles = shard.reshape(*dims[:dim], devices, dims[dim] // devices, *dims[dim + 1 :])
    return jnp.moveaxis(tiles, dim, 0)


def sent_and_summed(shard, axis, dim):
    devices = lax.axis_size(axis)
    tiles = lax.all_to_all(split_up(shard, dim, devices), axis, 0, 0, tiled=True)
    return jnp.sum(tiles, axis=0)


def gather_turned(arrays, axis, dims):
    turned = [jnp.moveaxis(a, dim, 0) for a, dim in zip(arrays, dims)]
    both = jnp.concatenate([t.reshape(len(t), -1) for t in turned], axis=1)
    filled, at, done = (lax.all_gather(both, axis, axis=0, tiled=True), 0, [])
    for t, dim in zip(turned, dims):
        slab = filled[:, at : at + t[0].size].reshape(-1, *t.shape[1:])
        done.append(jnp.moveaxis(slab, 0, dim))
        at += t[0].size
    return tuple(done)


def stacked_metrics(totals, horizon_tally, quantity_tally, grid_point_tally):
    block_rows = horizon_tally * quantity_tally
    width = totals.shape[1]
    error_power_two = (
        totals[:block_rows].reshape(horizon_tally, quantity_tally, width) / grid_point_tally
    )
    prediction_error = (
        totals[block_rows : 2 * block_rows].reshape(horizon_tally, quantity_tally, width)
        / grid_point_tally
    )
    paired_anomaly_term = (
        totals[2 * block_rows : 3 * block_rows].reshape(horizon_tally, quantity_tally, width)
        / grid_point_tally
    )
    predicted_spread_sum = (
        totals[3 * block_rows : 4 * block_rows].reshape(horizon_tally, quantity_tally, width)
        / grid_point_tally
    )
    observed_dispersion = (
        totals[4 * block_rows :].reshape(1, quantity_tally, width) / grid_point_tally
    )
    divisor_term = jnp.sqrt(
        jnp.maximum(predicted_spread_sum, minimum_divisor)
        * jnp.maximum(observed_dispersion, minimum_divisor)
    )
    return (error_power_two, prediction_error, paired_anomaly_term / divisor_term)


def local(
    prediction_fields, verifying_state, normal_state, evaluated_point_flag, parallels_each_strip
):
    horizon_tally, quantity_tally, zonal_circle_size, parallel_index = prediction_fields.shape
    lat_bands = lax.axis_size(LAT)
    lon_spokes = lax.axis_size(LON)
    lat_total = MEAN_ROWS * lat_bands + 1
    lon_total = zonal_circle_size * lon_spokes
    band_index = lax.axis_index(LAT)
    band_ids = jnp.arange(lat_bands, dtype=jnp.int32)
    first_row = jnp.sum(jnp.where(band_ids < band_index, parallels_each_strip, 0))
    band_filled = jnp.sum(jnp.where(band_ids == band_index, parallels_each_strip, 0))
    slot_ids = jnp.arange(parallel_index, dtype=jnp.int32)
    inside_band = slot_ids < band_filled
    angles = jnp.pi * jnp.arange(lat_total, dtype=jnp.float32) / (lat_total - 1)
    normalizer = jnp.sum(jnp.sin(angles))
    row_angle = jnp.pi * (first_row + slot_ids).astype(jnp.float32) / (lat_total - 1)
    area_factors = jnp.where(inside_band, jnp.sin(row_angle) * lat_total / normalizer, 0.0)
    retain_filter = (
        evaluated_point_flag.astype(jnp.float32) * inside_band.astype(jnp.float32)[None, :]
    )
    observed_anomaly = verifying_state - normal_state
    predicted_anomaly = prediction_fields - normal_state[None]
    mistake_field = predicted_anomaly - observed_anomaly[None]
    retained_entries = retain_filter[None, None]
    block_rows = horizon_tally * quantity_tally
    partial_value = jnp.concatenate(
        [
            jnp.sum(retained_entries * mistake_field * mistake_field, axis=2).reshape(
                block_rows, parallel_index
            ),
            jnp.sum(retained_entries * mistake_field, axis=2).reshape(block_rows, parallel_index),
            jnp.sum(retained_entries * predicted_anomaly * observed_anomaly[None], axis=2).reshape(
                block_rows, parallel_index
            ),
            jnp.sum(retained_entries * predicted_anomaly * predicted_anomaly, axis=2).reshape(
                block_rows, parallel_index
            ),
            jnp.sum(retain_filter[None] * observed_anomaly * observed_anomaly, axis=1),
        ],
        axis=0,
    )
    grand = by_axis(jnp.sum(partial_value * area_factors, axis=1), LAT_LON)
    shares = sent_and_summed(partial_value, LON, 1)
    scores = stacked_metrics(shares, horizon_tally, quantity_tally, float(lon_total))
    error_power_two, prediction_error, covariance_sum = gather_turned(
        (scores[0], scores[1], scores[2]), LON, (2, 2, 2)
    )
    total_square, total_offset, total_agree = stacked_metrics(
        grand[:, None], horizon_tally, quantity_tally, float(lat_total * lon_total)
    )
    rmse = jnp.sqrt(jnp.maximum(total_square[:, :, 0], minimum_divisor))
    return (
        error_power_two,
        prediction_error,
        covariance_sum,
        rmse,
        total_offset[:, :, 0],
        total_agree[:, :, 0],
    )


def solution(mesh):
    split = Mesh(mesh.devices.reshape(4, 2, 4, 8), ("lat_0", "lat_1", "lon_0", "lon_1"))
    placed = (P(None, None, LON, LAT), P(None, LON, LAT), P(None, LON, LAT), P(LON, LAT), P())
    return jax.shard_map(
        local,
        mesh=split,
        in_specs=placed,
        out_specs=(P(None, None, LAT), P(None, None, LAT), P(None, None, LAT), P(), P(), P()),
        check_vma=False,
    )
```

profile of v0, /device:TPU:8, one launch (start us, length us, event | category | flops | bytes accessed | tf_op | source)
XLA Modules:
  0.0 130.4 jit_solution(12620161045907325382)
XLA Ops:
  0.6 0.0 copy-start.3
  0.6 1.3 fusion.10
  1.9 0.6 compare_convert_fusion
  2.6 0.0 copy-start
  2.6 0.0 copy-start.2
  2.6 1.9 %copy.26 = f32[69,45,128]{2,1,0:T(8,128)S(1)} copy(f32[69,45,128]{2,0,1:T(8,128)} %param.7) | data formatting | bytes 3179520 | tf_op args[2]
  4.5 0.0 copy-done.3
  4.6 0.0 copy-done
  4.6 0.5 copy-done.2
  5.0 0.0 copy-start.1
  5.0 0.3 fusion.3
  5.4 0.3 copy.27
  5.7 2.2 %copy-done.1 = f32[4,69,45,128]{3,0,2,1:T(4,128)S(1)} copy-done((f32[4,69,45,128]{3,0,2,1:T(4,128)S(1)}, f32[4,69,45,128]{3,0,2,1:T(4,128)}, u32[]{:S(2)}) %copy-start.1) | copy-done | bytes 6359064
  7.8 10.2 %fusion.1 = (f32[4,69,128]{2,0,1:T(4,128)S(1)}, f32[4,69,128]{2,0,1:T(4,128)S(1)}, f32[4,69,128]{2,0,1:T(4,128)S(1)}, f32[4,69,128]{2,0,1:T(4,128)S(1)}) fusion(f32[4,69,45,128]{3,0,2,1:T(4,128)S(1)} %copy-done.1, f32[69,45,128]{2,1,0:T(8,128)S(1)} %copy.27, f32[69,45,128]{2,1,0:T(8,128)S(1)} %copy.26, f32[45,128]{1,0:T(8,128)S(1)} %convert_multiply_fusion), kind=kLoop, calls=%fused_computation.5 | loop fusion | flops 17346048 | bytes 10126848 | tf_op jit(solution)/shard_map/reduce_sum | solution.py:102
  18.0 0.2 copy.28
  18.2 0.2 concatenate.19
  18.4 0.2 copy.29
  18.6 0.2 concatenate.20
  18.8 0.2 copy.30
  19.0 0.2 concatenate.21
  19.2 0.2 copy.31
  19.4 0.2 concatenate.22
  19.6 0.1 copy.32
  19.7 1.5 %concatenate.24 = f32[1173,32,4]{0,2,1:T(4,128)} concatenate(f32[276,32,4]{0,2,1:T(4,128)S(1)} %concatenate.19, f32[276,32,4]{0,2,1:T(4,128)S(1)} %concatenate.20, f32[276,32,4]{0,2,1:T(4,128)S(1)} %concatenate.21, f32[276,32,4]{0,2,1:T(4,128)S(1)} %concatenate.22, f32[69,32,4]{0,2,1:T(4,128)S(1)} %bitcast.36), dimensions={0} | concatenate | bytes 1201152 | tf_op jit(solution)/shard_map/concatenate | solution.py:96
  21.2 11.7 %all-to-all-start = ((f32[32,1173,4]{1,2,0:T(4,128)}), f32[32,1173,4]{1,2,0:T(4,128)S(1)}, u32[]{:S(2)}, u32[]{:S(2)}) async-start(f32[32,1173,4]{1,2,0:T(4,128)} %bitcast.1), calls=%async_computation | async-start | bytes 1310720 | tf_op jit(solution)/shard_map/all_to_all | solution.py:27
  33.0 0.7 concatenate.26
  33.7 0.6 sine_reduce_fusion
  34.4 2.0 %compare_select_fusion.2 = f32[128]{0:T(128)S(1)} fusion(f32[]{:T(128)} %sine_reduce_fusion, s32[]{:T(128)} %get-tuple-element.22, s32[]{:T(128)} %get-tuple-element.23), kind=kLoop, calls=%fused_computation.31 | loop fusion | flops 896 | bytes 524 | tf_op jit(solution)/shard_map/jit(_where)/select_n | solution.py:87
  36.3 0.2 multiply_reduce_fusion.1
  36.6 10.6 %psum.28 = f32[1173]{0:T(1024)S(1)} all-reduce(f32[1173]{0:T(1024)S(1)} %multiply_reduce_fusion.1), channel_id=1, replica_groups=mesh['lat_0'=4,'lat_1'=2,'lon_0'=4,'lon_1'=8] {'lat_0'}, use_global_device_ids=true, to_apply=%region_10.11 | all-reduce | flops 1173 | bytes 9384 | tf_op jit(solution)/shard_map/psum | solution.py:16
  47.2 2.5 %psum.29 = f32[1173]{0:T(1024)S(1)} all-reduce(f32[1173]{0:T(1024)S(1)} %psum.28), channel_id=1, replica_groups=mesh['lat_0'=4,'lat_1'=2,'lon_0'=4,'lon_1'=8] {'lat_1'}, use_global_device_ids=true, to_apply=%region_11.12 | all-reduce | flops 1173 | bytes 9384 | tf_op jit(solution)/shard_map/psum | solution.py:16
  49.7 8.7 %psum.30 = f32[1173]{0:T(1024)S(1)} all-reduce(f32[1173]{0:T(1024)S(1)} %psum.29), channel_id=1, replica_groups=mesh['lat_0'=4,'lat_1'=2,'lon_0'=4,'lon_1'=8] {'lon_0'}, use_global_device_ids=true, to_apply=%region_12.13 | all-reduce | flops 1173 | bytes 9384 | tf_op jit(solution)/shard_map/psum | solution.py:16
  58.4 17.1 %psum.31 = f32[1173]{0:T(1024)S(1)} all-reduce(f32[1173]{0:T(1024)S(1)} %psum.30), channel_id=1, replica_groups=mesh['lat_0'=4,'lat_1'=2,'lon_0'=4,'lon_1'=8] {'lon_1'}, use_global_device_ids=true, to_apply=%region_13.14 | all-reduce | flops 1173 | bytes 9384 | tf_op jit(solution)/shard_map/psum | solution.py:16
  75.5 0.1 fusion.5
  75.6 0.1 div.94
  75.7 0.1 max.48
  75.8 0.7 div.92
  76.4 0.7 sqrt.14
  77.1 0.1 fusion.11
  77.2 0.6 rsqrt_multiply_fusion
  77.8 0.0 all-to-all-done
  77.8 0.1 reduce_sum.96
  77.9 0.1 slice_multiply_fusion.3
  77.9 0.1 fusion.8
  78.0 0.1 div.79
  78.1 0.1 max.42
  78.2 0.1 reshape.183
  78.3 0.1 div.75
  78.4 0.1 reshape.181
  78.5 0.1 div.77
  78.5 0.1 reshape.182
  78.6 0.1 maximum_bitcast_fusion
  78.7 48.9 %all-gather = f32[32,4,828]{2,1,0:T(4,128)S(1)} all-gather(f32[1,4,828]{2,1,0:T(4,128)S(1)} %maximum_bitcast_fusion), channel_id=1, replica_groups=mesh['lat_0'=4,'lat_1'=2,'lon_0'=4,'lon_1'=8] {'lon_0','lon_1'}, dimensions={0}, use_global_device_ids=true | all-gather | bytes 437184 | tf_op jit(solution)/shard_map/all_gather | solution.py:34
  127.6 0.2 reshape.192
  127.7 0.2 fusion.12
  127.9 0.1 copy.33
  128.0 0.7 copy.40
  128.7 0.1 copy.34
  128.8 0.7 copy.41
  129.5 0.1 copy.35
  129.7 0.7 copy.42
  (13 shorter events, 0.2 us)
Async XLA Ops:
  0.6 3.9 %copy-start.3 = (s32[45,128]{1,0:T(8,128)S(1)}, s32[45,128]{1,0:T(8,128)}, u32[]{:S(2)}) copy-start(s32[45,128]{1,0:T(8,128)} %param.8) | copy-start | bytes 69124
  2.6 2.0 %copy-start = (f32[69,45,128]{2,0,1:T(8,128)S(1)}, f32[69,45,128]{2,0,1:T(8,128)}, u32[]{:S(2)}) copy-start(f32[69,45,128]{2,0,1:T(8,128)} %param.7) | copy-start | bytes 4769284
  2.6 2.4 %copy-start.2 = (f32[69,45,128]{2,0,1:T(8,128)S(1)}, f32[69,45,128]{2,0,1:T(8,128)}, u32[]{:S(2)}) copy-start(f32[69,45,128]{2,0,1:T(8,128)} %param.6) | copy-start | bytes 4769284
  5.0 2.8 %copy-start.1 = (f32[4,69,45,128]{3,0,2,1:T(4,128)S(1)}, f32[4,69,45,128]{3,0,2,1:T(4,128)}, u32[]{:S(2)}) copy-start(f32[4,69,45,128]{3,0,2,1:T(4,128)} %param.5) | copy-start | bytes 19077124
  21.2 56.6 %all-to-all-start = ((f32[32,1173,4]{1,2,0:T(4,128)}), f32[32,1173,4]{1,2,0:T(4,128)S(1)}, u32[]{:S(2)}, u32[]{:S(2)}) async-start(f32[32,1173,4]{1,2,0:T(4,128)} %bitcast.1), calls=%async_computation | async-start | bytes 1310720 | tf_op jit(solution)/shard_map/all_to_all | solution.py:27
where the time goes:
time: 131 us; the launch traced here: 130 us
  blocking collectives  87.7 us (67%)
  other arithmetic  16.4 us (13%)
  local copies, waits for them, and re-layouts  13.6 us (10%)
  starting transfers between devices  11.7 us (9%)
    all_gather x1, blocking collectives, gather_turned(): filled, at, done = (lax.all_gather(both, axis, axis=0, tiled=True), 0, [])  48.9 us
    psum x4, blocking collectives, by_axis(): return functools.reduce(lax.psum, axes, shard)  38.9 us
    all_to_all x1, starting transfers between devices, sent_and_summed(): lax.all_to_all(split_up(shard, dim, devices), axis, 0, 0, tiled=True)  11.7 us
    reduce_sum x1, other arithmetic, local(): jnp.sum(retained_entries * predicted_anomaly * observed_anomaly[None], ax...  10.2 us
    unnamed x13, local copies, waits for them, and re-layouts  6.8 us
    concatenate x6, local copies, waits for them, and re-layouts, local(): jnp.concatenate([jnp.sum(retained_entries * mistake_field * mistake_field...  3.03 us
  transfers between devices with their start and end apart: 1, of which 0 were waited for; matrix products, arithmetic and copies ran while one was open for 5% of the time, Pallas kernels for 0%

commit v1 on v0

--- a/solution.py
+++ b/solution.py
@@ -31,7 +31,13 @@
 def gather_turned(arrays, axis, dims):
     turned = [jnp.moveaxis(a, dim, 0) for a, dim in zip(arrays, dims)]
     both = jnp.concatenate([t.reshape(len(t), -1) for t in turned], axis=1)
-    filled, at, done = (lax.all_gather(both, axis, axis=0, tiled=True), 0, [])
+
+    def play_yards(inner_x):
+        before = jnp.stack([inner_x] * jax.lax.axis_size(axis), axis=0)
+        part_next = jax.lax.all_to_all(before, axis, 0, 0)
+        return jnp.concatenate(part_next, 0)
+
+    filled, at, done = (play_yards(both), 0, [])
     for t, dim in zip(turned, dims):
         slab = filled[:, at : at + t[0].size].reshape(-1, *t.shape[1:])
         done.append(jnp.moveaxis(slab, 0, dim))

time: 131 us -> 105 us (0.80)
  blocking collectives: 87.7 us -> 38.9 us
  waiting for transfers between devices: 0.01 us -> 14.5 us
  starting transfers between devices: 11.7 us -> 19 us
    all_gather x1 -> x0, blocking collectives: 48.9 us -> none  [gather_turned(): filled, at, done = (lax.all_gather(both, axis, axis=0, tiled=True), 0, [])]
    all_to_all x1, waiting for transfers between devices: 0.01 us -> 14.5 us  [sent_and_summed(): lax.all_to_all(split_up(shard, dim, devices), axis, 0, 0, tiled=True)]
    all_to_all x0 -> x1, starting transfers between devices: none -> 7.31 us  [play_yards(): part_next = jax.lax.all_to_all(before, axis, 0, 0)]
    unnamed x13 -> x12, local copies, waits for them, and re-layouts: 6.8 us -> 6.64 us
  transfers between devices with their start and end apart: 1 -> 2, of which waited for: 0 -> 1; matrix products, arithmetic and copies ran while one was open for 5% -> 6% of each run, Pallas kernels for 0% -> 0%
where the time goes in v1:
time: 105 us; the launch traced here: 104 us
  blocking collectives  38.9 us (37%)
  starting transfers between devices  19 us (18%)
  other arithmetic  16.4 us (16%)
  waiting for transfers between devices  14.5 us (14%)
  local copies, waits for them, and re-layouts  14.4 us (14%)
    psum x4, blocking collectives, by_axis(): return functools.reduce(lax.psum, axes, shard)  38.9 us
    all_to_all x1, waiting for transfers between devices, sent_and_summed(): lax.all_to_all(split_up(shard, dim, devices), axis, 0, 0, tiled=True)  14.5 us
    all_to_all x1, starting transfers between devices, sent_and_summed(): lax.all_to_all(split_up(shard, dim, devices), axis, 0, 0, tiled=True)  11.7 us
    reduce_sum x1, other arithmetic, local(): jnp.sum(retained_entries * predicted_anomaly * observed_anomaly[None], ax...  10.2 us
    all_to_all x1, starting transfers between devices, play_yards(): part_next = jax.lax.all_to_all(before, axis, 0, 0)  7.31 us
    unnamed x12, local copies, waits for them, and re-layouts  6.64 us
    concatenate x6, local copies, waits for them, and re-layouts, local(): jnp.concatenate([jnp.sum(retained_entries * mistake_field * mistake_field...  3.03 us
  transfers between devices with their start and end apart: 2, of which 1 were waited for; matrix products, arithmetic and copies ran while one was open for 6% of the time, Pallas kernels for 0%

profile of v1, /device:TPU:8, one launch (start us, length us, event | category | flops | bytes accessed | tf_op | source)
XLA Modules:
  0.0 104.2 jit_solution(1039098703170629257)
XLA Ops:
  0.6 0.0 copy-start.3
  0.6 1.3 %fusion.10 = (s32[]{:T(128)}, s32[]{:T(128)}) fusion(s32[8]{0:T(128)} %param.9, s32[]{:T(128)S(6)} %add.21), kind=kLoop, calls=%fused_computation.34 | loop fusion | flops 46 | bytes 44 | tf_op jit(solution)/shard_map/reduce_sum | solution.py:86
  1.9 0.6 compare_convert_fusion
  2.6 0.0 copy-start
  2.6 0.0 copy-start.2
  2.6 1.9 %copy.27 = f32[69,45,128]{2,1,0:T(8,128)S(1)} copy(f32[69,45,128]{2,0,1:T(8,128)} %param.7) | data formatting | bytes 3179520 | tf_op args[2]
  4.5 0.0 copy-done.3
  4.6 0.0 copy-done
  4.6 0.5 copy-done.2
  5.0 0.0 copy-start.1
  5.0 0.3 fusion.3
  5.4 0.3 copy.28
  5.7 2.2 %copy-done.1 = f32[4,69,45,128]{3,0,2,1:T(4,128)S(1)} copy-done((f32[4,69,45,128]{3,0,2,1:T(4,128)S(1)}, f32[4,69,45,128]{3,0,2,1:T(4,128)}, u32[]{:S(2)}) %copy-start.1) | copy-done | bytes 6359064
  7.8 10.2 %fusion.1 = (f32[4,69,128]{2,0,1:T(4,128)S(1)}, f32[4,69,128]{2,0,1:T(4,128)S(1)}, f32[4,69,128]{2,0,1:T(4,128)S(1)}, f32[4,69,128]{2,0,1:T(4,128)S(1)}) fusion(f32[4,69,45,128]{3,0,2,1:T(4,128)S(1)} %copy-done.1, f32[69,45,128]{2,1,0:T(8,128)S(1)} %copy.28, f32[69,45,128]{2,1,0:T(8,128)S(1)} %copy.27, f32[45,128]{1,0:T(8,128)S(1)} %convert_multiply_fusion), kind=kLoop, calls=%fused_computation.5 | loop fusion | flops 17346048 | bytes 10126848 | tf_op jit(solution)/shard_map/reduce_sum | solution.py:108
  18.0 0.2 copy.29
  18.2 0.2 concatenate.19
  18.4 0.2 copy.30
  18.6 0.2 concatenate.20
  18.8 0.2 copy.31
  19.0 0.2 concatenate.21
  19.2 0.2 copy.32
  19.4 0.2 concatenate.22
  19.6 0.1 copy.33
  19.7 1.5 %concatenate.24 = f32[1173,32,4]{0,2,1:T(4,128)} concatenate(f32[276,32,4]{0,2,1:T(4,128)S(1)} %concatenate.19, f32[276,32,4]{0,2,1:T(4,128)S(1)} %concatenate.20, f32[276,32,4]{0,2,1:T(4,128)S(1)} %concatenate.21, f32[276,32,4]{0,2,1:T(4,128)S(1)} %concatenate.22, f32[69,32,4]{0,2,1:T(4,128)S(1)} %bitcast.34), dimensions={0} | concatenate | bytes 1201152 | tf_op jit(solution)/shard_map/concatenate | solution.py:102
  21.2 11.7 %all-to-all-start = ((f32[32,1173,4]{1,2,0:T(4,128)}), f32[32,1173,4]{1,2,0:T(4,128)S(1)}, u32[]{:S(2)}, u32[]{:S(2)}) async-start(f32[32,1173,4]{1,2,0:T(4,128)} %bitcast.1), calls=%async_computation | async-start | bytes 1310720 | tf_op jit(solution)/shard_map/all_to_all | solution.py:27
  33.0 0.7 concatenate.26
  33.7 0.6 sine_reduce_fusion
  34.4 2.0 %compare_select_fusion.2 = f32[128]{0:T(128)S(1)} fusion(f32[]{:T(128)} %sine_reduce_fusion, s32[]{:T(128)} %get-tuple-element.22, s32[]{:T(128)} %get-tuple-element.23), kind=kLoop, calls=%fused_computation.31 | loop fusion | flops 896 | bytes 524 | tf_op jit(solution)/shard_map/jit(_where)/select_n | solution.py:93
  36.3 14.5 %all-to-all-done = f32[32,1173,4]{1,2,0:T(4,128)S(1)} async-done(((f32[32,1173,4]{1,2,0:T(4,128)}), f32[32,1173,4]{1,2,0:T(4,128)S(1)}, u32[]{:S(2)}, u32[]{:S(2)}) %all-to-all-start) | async-done | bytes 600608 | tf_op jit(solution)/shard_map/all_to_all | solution.py:27
  50.9 0.1 reduce_sum.96
  51.0 0.1 slice_multiply_fusion.3
  51.0 0.1 fusion.8
  51.1 0.1 div.79
  51.2 0.1 max.42
  51.3 0.1 reshape.188
  51.4 0.1 div.75
  51.5 0.1 reshape.186
  51.6 0.1 div.77
  51.6 0.1 reshape.187
  51.7 0.1 pad_maximum_fusion
  51.8 0.8 stack.2
  52.7 7.3 %all-to-all-start.1 = ((f32[32,4,828]{2,1,0:T(4,128)}), f32[32,4,828]{2,1,0:T(4,128)S(1)}, u32[]{:S(2)}, u32[]{:S(2)}) async-start(f32[32,4,828]{2,1,0:T(4,128)} %stack.2), calls=%async_computation.1 | async-start | bytes 917504 | tf_op jit(solution)/shard_map/all_to_all | solution.py:37
  60.0 0.2 multiply_reduce_fusion.1
  60.2 10.6 %psum.28 = f32[1173]{0:T(1024)S(1)} all-reduce(f32[1173]{0:T(1024)S(1)} %multiply_reduce_fusion.1), channel_id=1, replica_groups=mesh['lat_0'=4,'lat_1'=2,'lon_0'=4,'lon_1'=8] {'lat_0'}, use_global_device_ids=true, to_apply=%region_10.11 | all-reduce | flops 1173 | bytes 9384 | tf_op jit(solution)/shard_map/psum | solution.py:16
  70.8 2.5 %psum.29 = f32[1173]{0:T(1024)S(1)} all-reduce(f32[1173]{0:T(1024)S(1)} %psum.28), channel_id=1, replica_groups=mesh['lat_0'=4,'lat_1'=2,'lon_0'=4,'lon_1'=8] {'lat_1'}, use_global_device_ids=true, to_apply=%region_11.12 | all-reduce | flops 1173 | bytes 9384 | tf_op jit(solution)/shard_map/psum | solution.py:16
  73.3 8.7 %psum.30 = f32[1173]{0:T(1024)S(1)} all-reduce(f32[1173]{0:T(1024)S(1)} %psum.29), channel_id=1, replica_groups=mesh['lat_0'=4,'lat_1'=2,'lon_0'=4,'lon_1'=8] {'lon_0'}, use_global_device_ids=true, to_apply=%region_12.13 | all-reduce | flops 1173 | bytes 9384 | tf_op jit(solution)/shard_map/psum | solution.py:16
  82.0 17.1 %psum.31 = f32[1173]{0:T(1024)S(1)} all-reduce(f32[1173]{0:T(1024)S(1)} %psum.30), channel_id=1, replica_groups=mesh['lat_0'=4,'lat_1'=2,'lon_0'=4,'lon_1'=8] {'lon_1'}, use_global_device_ids=true, to_apply=%region_13.14 | all-reduce | flops 1173 | bytes 9384 | tf_op jit(solution)/shard_map/psum | solution.py:16
  99.1 0.1 fusion.5
  99.2 0.1 div.94
  99.3 0.1 max.48
  99.4 0.7 div.92
  100.1 0.7 sqrt.14
  100.7 0.1 fusion.11
  100.8 0.6 rsqrt_multiply_fusion
  101.4 0.0 all-to-all-done.1
  101.4 0.2 reshape.189
  101.5 0.2 fusion.12
  101.7 0.1 copy.34
  101.8 0.7 copy.41
  102.5 0.1 copy.35
  102.7 0.7 copy.42
  103.4 0.1 copy.36
  103.5 0.7 copy.43
  (13 shorter events, 0.2 us)
Async XLA Ops:
  0.6 3.9 %copy-start.3 = (s32[45,128]{1,0:T(8,128)S(1)}, s32[45,128]{1,0:T(8,128)}, u32[]{:S(2)}) copy-start(s32[45,128]{1,0:T(8,128)} %param.8) | copy-start | bytes 69124
  2.6 2.0 %copy-start = (f32[69,45,128]{2,0,1:T(8,128)S(1)}, f32[69,45,128]{2,0,1:T(8,128)}, u32[]{:S(2)}) copy-start(f32[69,45,128]{2,0,1:T(8,128)} %param.7) | copy-start | bytes 4769284
  2.6 2.4 %copy-start.2 = (f32[69,45,128]{2,0,1:T(8,128)S(1)}, f32[69,45,128]{2,0,1:T(8,128)}, u32[]{:S(2)}) copy-start(f32[69,45,128]{2,0,1:T(8,128)} %param.6) | copy-start | bytes 4769284
  5.0 2.8 %copy-start.1 = (f32[4,69,45,128]{3,0,2,1:T(4,128)S(1)}, f32[4,69,45,128]{3,0,2,1:T(4,128)}, u32[]{:S(2)}) copy-start(f32[4,69,45,128]{3,0,2,1:T(4,128)} %param.5) | copy-start | bytes 19077124
  21.2 29.7 %all-to-all-start = ((f32[32,1173,4]{1,2,0:T(4,128)}), f32[32,1173,4]{1,2,0:T(4,128)S(1)}, u32[]{:S(2)}, u32[]{:S(2)}) async-start(f32[32,1173,4]{1,2,0:T(4,128)} %bitcast.1), calls=%async_computation | async-start | bytes 1310720 | tf_op jit(solution)/shard_map/all_to_all | solution.py:27
  52.7 48.7 %all-to-all-start.1 = ((f32[32,4,828]{2,1,0:T(4,128)}), f32[32,4,828]{2,1,0:T(4,128)S(1)}, u32[]{:S(2)}, u32[]{:S(2)}) async-start(f32[32,4,828]{2,1,0:T(4,128)} %stack.2), calls=%async_computation.1 | async-start | bytes 917504 | tf_op jit(solution)/shard_map/all_to_all | solution.py:37
